TPU v7x, 256 devices: a whole 4x4x8 slice. The times are simulated.
256 devices in a mesh: gx: 8 (over z), gy: 8 (over y, core), gz: 4 (over x).
Axes of the slice: x: 4, y: 4, z: 8, core: 2. Of those that a mesh axis runs over, the one named last changes fastest.
Arguments:
- density: float32 [64, 64, 512], P('gx', 'gy', 'gz'), may hold values from 0.5 to 2
- base_velocity: float32 [3, 64, 64, 512], P(None, 'gx', 'gy', 'gz'), may hold values from -0.4 to 0.4
- cells: int32 [3, 65536], P(None, ('gx', 'gy', 'gz')), may hold values from 0 to 511, as said below
- offsets: float32 [3, 65536], P(None, ('gx', 'gy', 'gz')), may hold values from 0 to 1
- target: float32 [3, 65536], P(None, ('gx', 'gy', 'gz')), may hold values from -0.4 to 0.4
- stiffness: float32 [65536], P(('gx', 'gy', 'gz')), may hold values from 0.01 to 0.1
- counts: int32 [256], P(('gx', 'gy', 'gz')), may hold values from 1 to 256, as said below
Outputs:
- forces: float32 [3, 65536], P(None, ('gx', 'gy', 'gz'))
Inputs may be any that keep to these rules, and one draw needn't show every extreme that they name: `cells`: each marker's cell lies inside the lattice block of the device that holds its slot. `counts`: some device holds exactly 256 live markers in every draw.
All inputs are finite; a program needn't handle non-finite values.
Results may differ from a plain program's by a relative error of at most 0.0001.
Values sent between devices are 32-bit elements; how exact they have to be, the bound alone decides.
A program may use at most 64 MiB of HBM per device.

v0:
```python
import jax
import jax.numpy as jnp
from jax import lax
from jax.sharding import Mesh
from jax.sharding import PartitionSpec as P

ITERS = 3
GY = ("gy_0", "gy_1")
GX_GY_GZ = ("gx", "gy_0", "gy_1", "gz")


def shifted(shard, axis, by):
    length = lax.axis_size(axis)
    return lax.ppermute(shard, axis, [(i, (i + by) % length) for i in range(length)])


def extended(cells, sides, width):
    for axis, dim in sides:
        count = lax.axis_size(axis)
        head = lax.slice_in_dim(cells, 0, width, axis=dim)
        tail = lax.slice_in_dim(cells, cells.shape[dim] - width, cells.shape[dim], axis=dim)
        cells = jnp.concatenate(
            [
                lax.ppermute(tail, axis, [(i, (i + 1) % count) for i in range(count)]),
                cells,
                lax.ppermute(head, axis, [((i + 1) % count, i) for i in range(count)]),
            ],
            axis=dim,
        )
    return cells


def one_axis_at_a_time(shard, axes):
    for axis in axes:
        shard = lax.psum(shard, axis)
    return shard


def moving_directions():
    listing = []
    for along_x in (-1, 0, 1):
        for along_y in (-1, 0, 1):
            for along_z in (-1, 0, 1):
                order = abs(along_x) + abs(along_y) + abs(along_z)
                if order == 1:
                    listing.append((along_x, along_y, along_z, 1.0 / 18.0))
                elif order == 2:
                    listing.append((along_x, along_y, along_z, 1.0 / 36.0))
    return listing


def delta_weights(fraction):

    def inner(radius):
        return (3.0 - 2.0 * radius + jnp.sqrt(1.0 + 4.0 * radius - 4.0 * radius * radius)) / 8.0

    def outer(radius):
        return (5.0 - 2.0 * radius - jnp.sqrt(-7.0 + 12.0 * radius - 4.0 * radius * radius)) / 8.0

    return jnp.stack(
        [outer(1.0 + fraction), inner(fraction), inner(1.0 - fraction), outer(2.0 - fraction)]
    )


def axis_rows(local, fraction, offset, extent):
    places = local[None, :] + jnp.arange(4, dtype=jnp.int32)[:, None] + offset
    hits = (places[:, :, None] == jnp.arange(extent, dtype=jnp.int32)[None, None, :]).astype(
        jnp.float32
    )
    return jnp.sum(delta_weights(fraction)[:, :, None] * hits, axis=0)


def make_tables(local, fractions, offset, extents):
    table_x = axis_rows(local[0], fractions[0], offset, extents[0]).T
    table_y = axis_rows(local[1], fractions[1], offset, extents[1]).T
    table_z = axis_rows(local[2], fractions[2], offset, extents[2])
    return (table_x, table_y, table_z)


def spread_dense(vector, tables):
    table_x, table_y, table_z = tables
    weighted = vector[:, None, None, :] * table_x[None, :, None, :] * table_y[None, None, :, :]
    return jnp.einsum("cxym,mz->cxyz", weighted, table_z, precision=lax.Precision.HIGHEST)


def interpolate_dense(field, tables):
    table_x, table_y, table_z = tables
    partial_rows = jnp.einsum("cxyz,mz->cxym", field, table_z, precision=lax.Precision.HIGHEST)
    return jnp.sum(partial_rows * (table_x[:, None, :] * table_y[None, :, :])[None], axis=(1, 2))


def surround(payload):
    stack = payload[None]
    tags = [(0, 0, 0)]
    pieces = [stack]
    grown = list(tags)
    for by in (-1, 1):
        pieces.append(shifted(stack, "gx", by))
        grown = grown + [(by, tag[1], tag[2]) for tag in tags]
    stack = jnp.concatenate(pieces, axis=0)
    tags = grown
    pieces = [stack]
    for by in (-1, 1):
        pieces.append(shifted(stack, GY, by))
        grown = grown + [(tag[0], by, tag[2]) for tag in tags]
    stack = jnp.concatenate(pieces, axis=0)
    tags = grown
    pieces = [stack]
    for by in (-1, 1):
        pieces.append(shifted(stack, "gz", by))
        grown = grown + [(tag[0], tag[1], by) for tag in tags]
    stack = jnp.concatenate(pieces, axis=0)
    return (stack, jnp.array(grown, dtype=jnp.int32))


def body(density, base_velocity, cells, offsets, target, stiffness, counts):
    size_x, size_y, size_z = density.shape
    capacity = cells.shape[1]
    anchor = jnp.stack(
        [lax.axis_index("gx") * size_x, lax.axis_index(GY) * size_y, lax.axis_index("gz") * size_z]
    )
    own_tables = make_tables(
        cells - anchor[:, None], offsets, 1, (size_x + 4, size_y + 4, size_z + 4)
    )
    live = (jnp.arange(capacity, dtype=jnp.int32) < counts[0]).astype(jnp.float32)
    scale = lax.rsqrt(density)
    stacked = jnp.concatenate([base_velocity, scale[None]], axis=0)
    fields = extended(stacked, (("gx", 1), (GY, 2), ("gz", 3)), 3)
    base_wide = fields[:3, 1 : size_x + 5, 1 : size_y + 5, 1 : size_z + 5]
    scale_wide = fields[3, 1 : size_x + 5, 1 : size_y + 5, 1 : size_z + 5]
    scale_full = fields[3]
    directions = moving_directions()
    block_sizes = jnp.array([size_x, size_y, size_z], dtype=jnp.int32)
    coordinates = (cells - anchor[:, None]).astype(jnp.float32)
    tables_all, tags = surround(jnp.concatenate([coordinates, offsets], axis=0))
    neighbour_local = (
        tables_all[:, :3].astype(jnp.int32) - (tags * block_sizes[None, :])[:, :, None]
    )
    neighbour_local = jnp.transpose(neighbour_local, (1, 0, 2)).reshape(3, -1)
    neighbour_fractions = jnp.transpose(tables_all[:, 3:], (1, 0, 2)).reshape(3, -1)
    neighbour_tables = make_tables(
        neighbour_local, neighbour_fractions, 2, (size_x + 6, size_y + 6, size_z + 6)
    )

    def spread_markers(vector):
        vectors_all, unused = surround(vector)
        flat_vectors = jnp.transpose(vectors_all, (1, 0, 2)).reshape(3, -1)
        return spread_dense(flat_vectors, neighbour_tables)

    def stream_wide(wide):
        post = jnp.zeros((3, size_x + 4, size_y + 4, size_z + 4), jnp.float32)
        for along_x, along_y, along_z, share in directions:
            piece = wide[
                :,
                1 - along_x : 5 - along_x + size_x,
                1 - along_y : 5 - along_y + size_y,
                1 - along_z : 5 - along_z + size_z,
            ]
            population = (
                3.0 * share * (along_x * piece[0] + along_y * piece[1] + along_z * piece[2])
            )
            post = post + jnp.stack(
                [along_x * population, along_y * population, along_z * population]
            )
        return scale_wide * (wide[:, 1 : size_x + 5, 1 : size_y + 5, 1 : size_z + 5] + post) * 0.5

    def apply(vector):
        wide = scale_full * spread_markers(vector)
        velocity_wide = stream_wide(wide)
        return live * (interpolate_dense(velocity_wide, own_tables) + stiffness * vector)

    def both_products(vector, image):
        return (
            one_axis_at_a_time(jnp.sum(vector * vector), GX_GY_GZ),
            one_axis_at_a_time(jnp.sum(vector * image), GX_GY_GZ),
        )

    right = live * (target - interpolate_dense(base_wide, own_tables))
    solution = jnp.zeros_like(right)
    residual = right
    image = apply(residual)
    norm_now, product = both_products(residual, image)
    alpha = norm_now / product
    direction = residual
    along = image
    for step in range(ITERS):
        solution = solution + alpha * direction
        residual = residual - alpha * along
        if step + 1 < ITERS:
            image = apply(residual)
            norm_next, product = both_products(residual, image)
            ratio = norm_next / norm_now
            alpha = norm_next / (product - ratio * norm_next / alpha)
            direction = residual + ratio * direction
            along = image + ratio * along
            norm_now = norm_next
    return solution


def solution(mesh):
    finer = Mesh(
        mesh.devices.reshape(mesh.shape["gx"], 4, 2, mesh.shape["gz"]), ("gx", "gy_0", "gy_1", "gz")
    )
    return jax.shard_map(
        body,
        mesh=finer,
        in_specs=(
            P("gx", GY, "gz"),
            P(None, "gx", GY, "gz"),
            P(None, GX_GY_GZ),
            P(None, GX_GY_GZ),
            P(None, GX_GY_GZ),
            P(GX_GY_GZ),
            P(GX_GY_GZ),
        ),
        out_specs=P(None, GX_GY_GZ),
        check_vma=False,
    )
```

profile of v0, /device:TPU:2, one launch (start us, length us, event | category | flops | bytes accessed | tf_op | source)
XLA Modules:
  0.0 327.5 jit_solution(7431941897793863222)
XLA Ops:
  0.1 0.8 fusion.530
  1.5 1.9 collective-permute-start.13
  3.4 4.0 %collective-permute-start.12 = (f32[1,6,256]{2,1,0:T(8,128)S(1)}, f32[1,6,256]{2,1,0:T(8,128)S(1)}, u32[]{:S(2)}, u32[]{:S(2)}) collective-permute-start(f32[1,6,256]{2,1,0:T(8,128)S(1)} %maximum_bitcast_fusion), channel_id=1, source_target_pairs={{0,224},{32,0},{64,32},{96,64},{128,96},{160,128},{192,160},{224,1... | collective-permute-start | bytes 18440 | tf_op jit(solution)/shard_map/ppermute | solution.py:14
  7.5 0.8 rsqrt_bitcast_fusion
  8.2 0.8 pad_maximum_fusion.7
  9.1 3.2 collective-permute-start.1
  12.3 0.9 subtract_multiply_fusion.12
  15.2 2.9 collective-permute-start.14
  18.2 1.5 collective-permute-done.14
  19.7 1.6 collective-permute-start.17
  22.0 0.9 pad_maximum_fusion.2
  22.9 2.9 collective-permute-start.3
  26.0 0.8 fusion.451
  28.8 34.5 %select_reduce_fusion = f32[6912,134]{0,1:T(8,128)S(1)} fusion(f32[4,6912]{1,0:T(4,128)S(1)} %pad_maximum_fusion.5, s32[4,6912]{1,0:T(4,128)S(1)} %add_add_fusion), kind=kLoop, calls=%fused_computation.6 | loop fusion | flops 10188288 | bytes 3926016 | tf_op jit(solution)/shard_map/reduce_sum | solution.py:70
  63.6 1.0 select_reduce_fusion.1
  64.9 1.6 collective-permute-start.4
  67.0 1.0 select_reduce_fusion.2
  68.0 8.6 %collective-permute-done.4 = f32[4,14,14,3]{3,2,1,0:T(8,128)S(1)} collective-permute-done((f32[4,14,14,3]{3,2,1,0:T(8,128)S(1)}, f32[4,14,14,3]{3,2,1,0:T(8,128)S(1)}, u32[]{:S(2)}, u32[]{:S(2)}) %collective-permute-start.4) | collective-permute-done | bytes 9440 | tf_op jit(solution)/shard_map/ppermute | solution.py:24
  76.6 0.9 collective-permute-done.5
  79.0 3.2 collective-permute-start.6
  82.3 1.6 collective-permute-done.7
  83.9 2.9 collective-permute-start.8
  86.8 1.4 collective-permute-done.8
  88.3 1.0 collective-permute-start.10
  89.4 1.6 collective-permute-start.11
  91.0 1.5 collective-permute-done.10
  92.5 2.2 collective-permute-done.11
  94.9 14.8 %fusion.15 = f32[3,14,14,134]{3,2,1,0:T(8,128)S(1)} fusion(f32[6912,134]{0,1:T(8,128)S(1)} %select_reduce_fusion, f32[14,6912]{1,0:T(8,128)S(1)} %bitcast.78, f32[3,14,6912]{2,1,0:T(8,128)S(1)} %broadcast_multiply_fusion.2, f32[14,14,134]{2,1,0:T(8,128)S(1)} %slice_bitcast_fusion), kind=kOutput, calls=%fused_computation.21 | convolution fusion | flops 6539466752 | bytes 5673344 | tf_op jit(solution)/shard_map/cxym,mz->cxyz/dot_general | solution.py:83
  110.4 1.0 broadcast_multiply_fusion.30
  112.7 0.8 broadcast_multiply_fusion.32
  113.8 1.7 fusion.31
  116.3 18.0 %all-reduce.2 = (f32[]{:T(128)}, f32[]{:T(128)}) all-reduce(f32[]{:T(128)} %get-tuple-element.13, f32[]{:T(128)} %get-tuple-element.12), channel_id=1, replica_groups=mesh['gx'=8,'gy_0'=4,'gy_1'=2,'gz'=4] {'gx'}, use_global_device_ids=true, to_apply=%region_5.0 | all-reduce | flops 2 | bytes 16 | tf_op jit(solution)/shard_map/psum | solution.py:35
  134.3 10.3 %all-reduce.8 = (f32[]{:T(128)}, f32[]{:T(128)}) all-reduce(f32[]{:T(128)} %get-tuple-element.18, f32[]{:T(128)} %get-tuple-element.19), channel_id=1, replica_groups=mesh['gx'=8,'gy_0'=4,'gy_1'=2,'gz'=4] {'gy_0'}, use_global_device_ids=true, to_apply=%region_6.0 | all-reduce | flops 2 | bytes 16 | tf_op jit(solution)/shard_map/psum | solution.py:35
  144.6 3.1 all-reduce.11
  147.7 11.8 %all-reduce.5 = (f32[]{:T(128)}, f32[]{:T(128)}) all-reduce(f32[]{:T(128)} %get-tuple-element.36, f32[]{:T(128)} %get-tuple-element.37), channel_id=1, replica_groups=mesh['gx'=8,'gy_0'=4,'gy_1'=2,'gz'=4] {'gz'}, use_global_device_ids=true, to_apply=%region_8.0 | all-reduce | flops 2 | bytes 16 | tf_op jit(solution)/shard_map/psum | solution.py:35
  160.9 3.2 collective-permute-start.18
  164.1 1.6 collective-permute-done.19
  165.7 2.9 collective-permute-start.20
  168.7 1.4 collective-permute-done.20
  170.2 2.2 collective-permute-start.23
  172.4 1.7 collective-permute-done.22
  174.5 17.1 %fusion.20 = f32[3,14,14,134]{3,2,1,0:T(8,128)S(1)} fusion(f32[6912,134]{0,1:T(8,128)} %copy-done, f32[3,14,6912]{2,1,0:T(8,128)S(1)} %broadcast_multiply_fusion.1, f32[14,6912]{1,0:T(8,128)S(1)} %bitcast.79, f32[14,14,134]{2,1,0:T(8,128)S(1)} %slice_bitcast_fusion), kind=kOutput, calls=%fused_computation.22 | convolution fusion | flops 6539466752 | bytes 5673344 | tf_op jit(solution)/shard_map/cxym,mz->cxyz/dot_general | solution.py:83
  192.3 1.0 broadcast_multiply_fusion.21
  193.9 0.7 broadcast_multiply_fusion.95
  194.6 0.8 broadcast_multiply_fusion.23
  195.8 1.7 fusion.32
  198.1 18.1 %all-reduce.1 = (f32[]{:T(128)}, f32[]{:T(128)}) all-reduce(f32[]{:T(128)} %get-tuple-element.11, f32[]{:T(128)} %get-tuple-element.10), channel_id=1, replica_groups=mesh['gx'=8,'gy_0'=4,'gy_1'=2,'gz'=4] {'gx'}, use_global_device_ids=true, to_apply=%region_19.0 | all-reduce | flops 2 | bytes 16 | tf_op jit(solution)/shard_map/psum | solution.py:35
  216.2 8.4 %all-reduce.7 = (f32[]{:T(128)}, f32[]{:T(128)}) all-reduce(f32[]{:T(128)} %get-tuple-element.16, f32[]{:T(128)} %get-tuple-element.17), channel_id=1, replica_groups=mesh['gx'=8,'gy_0'=4,'gy_1'=2,'gz'=4] {'gy_0'}, use_global_device_ids=true, to_apply=%region_20.0 | all-reduce | flops 2 | bytes 16 | tf_op jit(solution)/shard_map/psum | solution.py:35
  224.5 3.1 all-reduce.10
  227.6 11.5 %all-reduce.4 = (f32[]{:T(128)}, f32[]{:T(128)}) all-reduce(f32[]{:T(128)} %get-tuple-element.34, f32[]{:T(128)} %get-tuple-element.35), channel_id=1, replica_groups=mesh['gx'=8,'gy_0'=4,'gy_1'=2,'gz'=4] {'gz'}, use_global_device_ids=true, to_apply=%region_22.0 | all-reduce | flops 2 | bytes 16 | tf_op jit(solution)/shard_map/psum | solution.py:35
  243.9 3.2 collective-permute-start.24
  247.1 1.6 collective-permute-done.25
  248.7 2.9 collective-permute-start.26
  251.7 1.4 collective-permute-done.26
  253.2 2.2 collective-permute-start.29
  255.4 2.1 collective-permute-done.28
  257.8 16.9 %fusion.25 = f32[3,14,14,134]{3,2,1,0:T(8,128)S(1)} fusion(f32[6912,134]{0,1:T(8,128)} %copy-done, f32[3,14,6912]{2,1,0:T(8,128)S(1)} %broadcast_multiply_fusion, f32[14,6912]{1,0:T(8,128)S(1)} %bitcast.80, f32[14,14,134]{2,1,0:T(8,128)S(1)} %slice_bitcast_fusion), kind=kOutput, calls=%fused_computation.23 | convolution fusion | flops 6539466752 | bytes 5673344 | tf_op jit(solution)/shard_map/cxym,mz->cxyz/dot_general | solution.py:83
  275.4 1.0 broadcast_multiply_fusion.12
  277.7 0.8 broadcast_multiply_fusion.14
  278.8 1.7 fusion.33
  281.2 18.0 %all-reduce = (f32[]{:T(128)}, f32[]{:T(128)}) all-reduce(f32[]{:T(128)} %get-tuple-element.9, f32[]{:T(128)} %get-tuple-element.8), channel_id=1, replica_groups=mesh['gx'=8,'gy_0'=4,'gy_1'=2,'gz'=4] {'gx'}, use_global_device_ids=true, to_apply=%region_30.0 | all-reduce | flops 2 | bytes 16 | tf_op jit(solution)/shard_map/psum | solution.py:35
  299.2 8.9 %all-reduce.6 = (f32[]{:T(128)}, f32[]{:T(128)}) all-reduce(f32[]{:T(128)} %get-tuple-element.14, f32[]{:T(128)} %get-tuple-element.15), channel_id=1, replica_groups=mesh['gx'=8,'gy_0'=4,'gy_1'=2,'gz'=4] {'gy_0'}, use_global_device_ids=true, to_apply=%region_31.0 | all-reduce | flops 2 | bytes 16 | tf_op jit(solution)/shard_map/psum | solution.py:35
  308.1 3.1 all-reduce.9
  311.2 11.5 %all-reduce.3 = (f32[]{:T(128)}, f32[]{:T(128)}) all-reduce(f32[]{:T(128)} %get-tuple-element.32, f32[]{:T(128)} %get-tuple-element.33), channel_id=1, replica_groups=mesh['gx'=8,'gy_0'=4,'gy_1'=2,'gz'=4] {'gz'}, use_global_device_ids=true, to_apply=%region_33.0 | all-reduce | flops 2 | bytes 16 | tf_op jit(solution)/shard_map/psum | solution.py:35
  (141 shorter events, 17.5 us)
Async XLA Ops:
  1.5 13.6 %collective-permute-start.13 = (f32[1,6,256]{2,1,0:T(8,128)S(1)}, f32[1,6,256]{2,1,0:T(8,128)S(1)}, u32[]{:S(2)}, u32[]{:S(2)}) collective-permute-start(f32[1,6,256]{2,1,0:T(8,128)S(1)} %maximum_bitcast_fusion), channel_id=1, source_target_pairs={{0,32},{32,64},{64,96},{96,128},{128,160},{160,192},{192,224},{224... | collective-permute-start | bytes 18440 | tf_op jit(solution)/shard_map/ppermute | solution.py:14
  3.4 11.7 %collective-permute-start.12 = (f32[1,6,256]{2,1,0:T(8,128)S(1)}, f32[1,6,256]{2,1,0:T(8,128)S(1)}, u32[]{:S(2)}, u32[]{:S(2)}) collective-permute-start(f32[1,6,256]{2,1,0:T(8,128)S(1)} %maximum_bitcast_fusion), channel_id=1, source_target_pairs={{0,224},{32,0},{64,32},{96,64},{128,96},{160,128},{192,160},{224,1... | collective-permute-start | bytes 18440 | tf_op jit(solution)/shard_map/ppermute | solution.py:14
  9.0 12.9 %collective-permute-start = (f32[4,3,8,128]{3,2,1,0:T(8,128)S(1)}, f32[4,3,8,128]{3,2,1,0:T(8,128)S(1)}, u32[]{:S(2)}, u32[]{:S(2)}) collective-permute-start(f32[4,3,8,128]{3,2,1,0:T(8,128)S(1)} %get-tuple-element.221), channel_id=1, source_target_pairs={{0,32},{32,64},{64,96},{96,128},{128,160},{160,192},{192,224},{224... | collective-permute-start | bytes 147464 | tf_op jit(solution)/shard_map/ppermute | solution.py:24
  9.1 12.8 %collective-permute-start.1 = (f32[4,3,8,128]{3,2,1,0:T(8,128)S(1)}, f32[4,3,8,128]{3,2,1,0:T(8,128)S(1)}, u32[]{:S(2)}, u32[]{:S(2)}) collective-permute-start(f32[4,3,8,128]{3,2,1,0:T(8,128)S(1)} %get-tuple-element.222), channel_id=1, source_target_pairs={{32,0},{64,32},{96,64},{128,96},{160,128},{192,160},{224,192},{0,2... | collective-permute-start | bytes 147464 | tf_op jit(solution)/shard_map/ppermute | solution.py:26
  15.2 4.5 %collective-permute-start.15 = (f32[3,6,256]{2,1,0:T(8,128)S(1)}, f32[3,6,256]{2,1,0:T(8,128)S(1)}, u32[]{:S(2)}, u32[]{:S(2)}) collective-permute-start(f32[3,6,256]{2,1,0:T(8,128)S(1)} %pad_maximum_fusion.8), channel_id=1, source_target_pairs={{0,4},{4,8},{8,12},{12,16},{16,20},{20,24},{24,28},{28,0},{1,5},{5... | collective-permute-start | bytes 55304 | tf_op jit(solution)/shard_map/ppermute | solution.py:14
  15.2 4.5 %collective-permute-start.14 = (f32[3,6,256]{2,1,0:T(8,128)S(1)}, f32[3,6,256]{2,1,0:T(8,128)S(1)}, u32[]{:S(2)}, u32[]{:S(2)}) collective-permute-start(f32[3,6,256]{2,1,0:T(8,128)S(1)} %pad_maximum_fusion.8), channel_id=1, source_target_pairs={{0,28},{4,0},{8,4},{12,8},{16,12},{20,16},{24,20},{28,24},{1,29},{... | collective-permute-start | bytes 55304 | tf_op jit(solution)/shard_map/ppermute | solution.py:14
  19.7 6.2 %collective-permute-start.17 = (f32[9,6,256]{2,1,0:T(8,128)S(1)}, f32[9,6,256]{2,1,0:T(8,128)S(1)}, u32[]{:S(2)}, u32[]{:S(2)}) collective-permute-start(f32[9,6,256]{2,1,0:T(8,128)S(1)} %get-tuple-element.238), channel_id=1, source_target_pairs={{0,1},{1,2},{2,3},{3,0},{4,5},{5,6},{6,7},{7,4},{8,9},{9,10},{10,1... | collective-permute-start | bytes 165896 | tf_op jit(solution)/shard_map/ppermute | solution.py:14
  21.3 4.6 %collective-permute-start.16 = (f32[9,6,256]{2,1,0:T(8,128)S(1)}, f32[9,6,256]{2,1,0:T(8,128)S(1)}, u32[]{:S(2)}, u32[]{:S(2)}) collective-permute-start(f32[9,6,256]{2,1,0:T(8,128)S(1)} %get-tuple-element.238), channel_id=1, source_target_pairs={{0,3},{1,0},{2,1},{3,2},{4,7},{5,4},{6,5},{7,6},{8,11},{9,8},{10,9... | collective-permute-start | bytes 165896 | tf_op jit(solution)/shard_map/ppermute | solution.py:14
  22.9 41.7 %collective-permute-start.2 = (f32[4,14,3,128]{3,2,1,0:T(4,128)S(1)}, f32[4,14,3,128]{3,2,1,0:T(4,128)S(1)}, u32[]{:S(2)}, u32[]{:S(2)}) collective-permute-start(f32[4,14,3,128]{3,2,1,0:T(4,128)S(1)} %get-tuple-element.183), channel_id=1, source_target_pairs={{0,4},{4,8},{8,12},{12,16},{16,20},{20,24},{24,28},{28,0},{1,5},{5... | collective-permute-start | bytes 258056 | tf_op jit(solution)/shard_map/ppermute | solution.py:24
  22.9 41.7 %collective-permute-start.3 = (f32[4,14,3,128]{3,2,1,0:T(4,128)S(1)}, f32[4,14,3,128]{3,2,1,0:T(4,128)S(1)}, u32[]{:S(2)}, u32[]{:S(2)}) collective-permute-start(f32[4,14,3,128]{3,2,1,0:T(4,128)S(1)} %get-tuple-element.184), channel_id=1, source_target_pairs={{4,0},{8,4},{12,8},{16,12},{20,16},{24,20},{28,24},{0,28},{5,1},{9... | collective-permute-start | bytes 258056 | tf_op jit(solution)/shard_map/ppermute | solution.py:26
  25.9 38.7 %copy-start.1 = (f32[3,8,8,128]{3,2,1,0:T(8,128)S(1)}, f32[3,8,8,128]{3,2,1,0:T(8,128)}, u32[]{:S(2)}) copy-start(f32[3,8,8,128]{3,2,1,0:T(8,128)} %param.10) | copy-start | bytes 294916
  63.3 31.6 %copy-start = (f32[6912,134]{0,1:T(8,128)}, f32[6912,134]{0,1:T(8,128)S(1)}, u32[]{:S(2)}) copy-start(f32[6912,134]{0,1:T(8,128)S(1)} %select_reduce_fusion) | copy-start | bytes 11114500
  63.6 15.4 %copy-start.3 = (f32[3,256]{1,0:T(4,128)S(1)}, f32[3,256]{1,0:T(4,128)}, u32[]{:S(2)}) copy-start(f32[3,256]{1,0:T(4,128)} %param.13) | copy-start | bytes 9220
  64.9 11.7 %collective-permute-start.4 = (f32[4,14,14,3]{3,2,1,0:T(8,128)S(1)}, f32[4,14,14,3]{3,2,1,0:T(8,128)S(1)}, u32[]{:S(2)}, u32[]{:S(2)}) collective-permute-start(f32[4,14,14,3]{3,2,1,0:T(8,128)S(1)} %get-tuple-element.181), channel_id=1, source_target_pairs={{0,1},{1,2},{2,3},{3,0},{4,5},{5,6},{6,7},{7,4},{8,9},{9,10},{10,1... | collective-permute-start | bytes 28232 | tf_op jit(solution)/shard_map/ppermute | solution.py:24
  66.5 11.1 %collective-permute-start.5 = (f32[4,14,14,3]{3,2,1,0:T(8,128)S(1)}, f32[4,14,14,3]{3,2,1,0:T(8,128)S(1)}, u32[]{:S(2)}, u32[]{:S(2)}) collective-permute-start(f32[4,14,14,3]{3,2,1,0:T(8,128)S(1)} %get-tuple-element.182), channel_id=1, source_target_pairs={{1,0},{2,1},{3,2},{0,3},{5,4},{6,5},{7,6},{4,7},{9,8},{10,9},{11,1... | collective-permute-start | bytes 28232 | tf_op jit(solution)/shard_map/ppermute | solution.py:26
  79.0 4.9 %collective-permute-start.7 = (f32[1,3,256]{2,1,0:T(4,128)S(1)}, f32[1,3,256]{2,1,0:T(4,128)S(1)}, u32[]{:S(2)}, u32[]{:S(2)}) collective-permute-start(f32[1,3,256]{2,1,0:T(4,128)S(1)} %bitcast.81), channel_id=1, source_target_pairs={{0,32},{32,64},{64,96},{96,128},{128,160},{160,192},{192,224},{224... | collective-permute-start | bytes 9224 | tf_op jit(solution)/shard_map/ppermute | solution.py:14
  79.0 4.8 %collective-permute-start.6 = (f32[1,3,256]{2,1,0:T(4,128)S(1)}, f32[1,3,256]{2,1,0:T(4,128)S(1)}, u32[]{:S(2)}, u32[]{:S(2)}) collective-permute-start(f32[1,3,256]{2,1,0:T(4,128)S(1)} %bitcast.82), channel_id=1, source_target_pairs={{0,224},{32,0},{64,32},{96,64},{128,96},{160,128},{192,160},{224,1... | collective-permute-start | bytes 9224 | tf_op jit(solution)/shard_map/ppermute | solution.py:14
  83.9 4.4 %collective-permute-start.9 = (f32[3,3,256]{2,1,0:T(4,128)S(1)}, f32[3,3,256]{2,1,0:T(4,128)S(1)}, u32[]{:S(2)}, u32[]{:S(2)}) collective-permute-start(f32[3,3,256]{2,1,0:T(4,128)S(1)} %pad_maximum_fusion.9), channel_id=1, source_target_pairs={{0,4},{4,8},{8,12},{12,16},{16,20},{20,24},{24,28},{28,0},{1,5},{5... | collective-permute-start | bytes 27656 | tf_op jit(solution)/shard_map/ppermute | solution.py:14
  83.9 4.3 %collective-permute-start.8 = (f32[3,3,256]{2,1,0:T(4,128)S(1)}, f32[3,3,256]{2,1,0:T(4,128)S(1)}, u32[]{:S(2)}, u32[]{:S(2)}) collective-permute-start(f32[3,3,256]{2,1,0:T(4,128)S(1)} %pad_maximum_fusion.9), channel_id=1, source_target_pairs={{0,28},{4,0},{8,4},{12,8},{16,12},{20,16},{24,20},{28,24},{1,29},{... | collective-permute-start | bytes 27656 | tf_op jit(solution)/shard_map/ppermute | solution.py:14
  88.3 4.3 %collective-permute-start.10 = (f32[9,3,256]{2,1,0:T(4,128)S(1)}, f32[9,3,256]{2,1,0:T(4,128)S(1)}, u32[]{:S(2)}, u32[]{:S(2)}) collective-permute-start(f32[9,3,256]{2,1,0:T(4,128)S(1)} %get-tuple-element.250), channel_id=1, source_target_pairs={{0,3},{1,0},{2,1},{3,2},{4,7},{5,4},{6,5},{7,6},{8,11},{9,8},{10,9... | collective-permute-start | bytes 82952 | tf_op jit(solution)/shard_map/ppermute | solution.py:14
  89.4 5.4 %collective-permute-start.11 = (f32[9,3,256]{2,1,0:T(4,128)S(1)}, f32[9,3,256]{2,1,0:T(4,128)S(1)}, u32[]{:S(2)}, u32[]{:S(2)}) collective-permute-start(f32[9,3,256]{2,1,0:T(4,128)S(1)} %get-tuple-element.250), channel_id=1, source_target_pairs={{0,1},{1,2},{2,3},{3,0},{4,5},{5,6},{6,7},{7,4},{8,9},{9,10},{10,1... | collective-permute-start | bytes 82952 | tf_op jit(solution)/shard_map/ppermute | solution.py:14
  113.8 1.7 copy-start.2
  160.8 4.9 %collective-permute-start.19 = (f32[1,3,256]{2,1,0:T(4,128)S(1)}, f32[1,3,256]{2,1,0:T(4,128)S(1)}, u32[]{:S(2)}, u32[]{:S(2)}) collective-permute-start(f32[1,3,256]{2,1,0:T(4,128)S(1)} %bitcast.84), channel_id=1, source_target_pairs={{0,32},{32,64},{64,96},{96,128},{128,160},{160,192},{192,224},{224... | collective-permute-start | bytes 9224 | tf_op jit(solution)/shard_map/ppermute | solution.py:14
  160.9 4.8 %collective-permute-start.18 = (f32[1,3,256]{2,1,0:T(4,128)S(1)}, f32[1,3,256]{2,1,0:T(4,128)S(1)}, u32[]{:S(2)}, u32[]{:S(2)}) collective-permute-start(f32[1,3,256]{2,1,0:T(4,128)S(1)} %bitcast.85), channel_id=1, source_target_pairs={{0,224},{32,0},{64,32},{96,64},{128,96},{160,128},{192,160},{224,1... | collective-permute-start | bytes 9224 | tf_op jit(solution)/shard_map/ppermute | solution.py:14
  165.7 4.4 %collective-permute-start.21 = (f32[3,3,256]{2,1,0:T(4,128)S(1)}, f32[3,3,256]{2,1,0:T(4,128)S(1)}, u32[]{:S(2)}, u32[]{:S(2)}) collective-permute-start(f32[3,3,256]{2,1,0:T(4,128)S(1)} %pad_maximum_fusion.10), channel_id=1, source_target_pairs={{0,4},{4,8},{8,12},{12,16},{16,20},{20,24},{24,28},{28,0},{1,5},{5... | collective-permute-start | bytes 27656 | tf_op jit(solution)/shard_map/ppermute | solution.py:14
  165.7 4.3 %collective-permute-start.20 = (f32[3,3,256]{2,1,0:T(4,128)S(1)}, f32[3,3,256]{2,1,0:T(4,128)S(1)}, u32[]{:S(2)}, u32[]{:S(2)}) collective-permute-start(f32[3,3,256]{2,1,0:T(4,128)S(1)} %pad_maximum_fusion.10), channel_id=1, source_target_pairs={{0,28},{4,0},{8,4},{12,8},{16,12},{20,16},{24,20},{28,24},{1,29},{... | collective-permute-start | bytes 27656 | tf_op jit(solution)/shard_map/ppermute | solution.py:14
  170.1 4.0 %collective-permute-start.22 = (f32[9,3,256]{2,1,0:T(4,128)S(1)}, f32[9,3,256]{2,1,0:T(4,128)S(1)}, u32[]{:S(2)}, u32[]{:S(2)}) collective-permute-start(f32[9,3,256]{2,1,0:T(4,128)S(1)} %get-tuple-element.246), channel_id=1, source_target_pairs={{0,3},{1,0},{2,1},{3,2},{4,7},{5,4},{6,5},{7,6},{8,11},{9,8},{10,9... | collective-permute-start | bytes 82952 | tf_op jit(solution)/shard_map/ppermute | solution.py:14
  170.2 4.2 %collective-permute-start.23 = (f32[9,3,256]{2,1,0:T(4,128)S(1)}, f32[9,3,256]{2,1,0:T(4,128)S(1)}, u32[]{:S(2)}, u32[]{:S(2)}) collective-permute-start(f32[9,3,256]{2,1,0:T(4,128)S(1)} %get-tuple-element.246), channel_id=1, source_target_pairs={{0,1},{1,2},{2,3},{3,0},{4,5},{5,6},{6,7},{7,4},{8,9},{9,10},{10,1... | collective-permute-start | bytes 82952 | tf_op jit(solution)/shard_map/ppermute | solution.py:14
  243.8 4.9 %collective-permute-start.25 = (f32[1,3,256]{2,1,0:T(4,128)S(1)}, f32[1,3,256]{2,1,0:T(4,128)S(1)}, u32[]{:S(2)}, u32[]{:S(2)}) collective-permute-start(f32[1,3,256]{2,1,0:T(4,128)S(1)} %bitcast.93), channel_id=1, source_target_pairs={{0,32},{32,64},{64,96},{96,128},{128,160},{160,192},{192,224},{224... | collective-permute-start | bytes 9224 | tf_op jit(solution)/shard_map/ppermute | solution.py:14
  243.9 4.8 %collective-permute-start.24 = (f32[1,3,256]{2,1,0:T(4,128)S(1)}, f32[1,3,256]{2,1,0:T(4,128)S(1)}, u32[]{:S(2)}, u32[]{:S(2)}) collective-permute-start(f32[1,3,256]{2,1,0:T(4,128)S(1)} %bitcast.94), channel_id=1, source_target_pairs={{0,224},{32,0},{64,32},{96,64},{128,96},{160,128},{192,160},{224,1... | collective-permute-start | bytes 9224 | tf_op jit(solution)/shard_map/ppermute | solution.py:14
  248.7 4.4 %collective-permute-start.27 = (f32[3,3,256]{2,1,0:T(4,128)S(1)}, f32[3,3,256]{2,1,0:T(4,128)S(1)}, u32[]{:S(2)}, u32[]{:S(2)}) collective-permute-start(f32[3,3,256]{2,1,0:T(4,128)S(1)} %pad_maximum_fusion.11), channel_id=1, source_target_pairs={{0,4},{4,8},{8,12},{12,16},{16,20},{20,24},{24,28},{28,0},{1,5},{5... | collective-permute-start | bytes 27656 | tf_op jit(solution)/shard_map/ppermute | solution.py:14
  248.7 4.3 %collective-permute-start.26 = (f32[3,3,256]{2,1,0:T(4,128)S(1)}, f32[3,3,256]{2,1,0:T(4,128)S(1)}, u32[]{:S(2)}, u32[]{:S(2)}) collective-permute-start(f32[3,3,256]{2,1,0:T(4,128)S(1)} %pad_maximum_fusion.11), channel_id=1, source_target_pairs={{0,28},{4,0},{8,4},{12,8},{16,12},{20,16},{24,20},{28,24},{1,29},{... | collective-permute-start | bytes 27656 | tf_op jit(solution)/shard_map/ppermute | solution.py:14
  253.1 4.3 %collective-permute-start.28 = (f32[9,3,256]{2,1,0:T(4,128)S(1)}, f32[9,3,256]{2,1,0:T(4,128)S(1)}, u32[]{:S(2)}, u32[]{:S(2)}) collective-permute-start(f32[9,3,256]{2,1,0:T(4,128)S(1)} %get-tuple-element.242), channel_id=1, source_target_pairs={{0,3},{1,0},{2,1},{3,2},{4,7},{5,4},{6,5},{7,6},{8,11},{9,8},{10,9... | collective-permute-start | bytes 82952 | tf_op jit(solution)/shard_map/ppermute | solution.py:14
  253.2 4.5 %collective-permute-start.29 = (f32[9,3,256]{2,1,0:T(4,128)S(1)}, f32[9,3,256]{2,1,0:T(4,128)S(1)}, u32[]{:S(2)}, u32[]{:S(2)}) collective-permute-start(f32[9,3,256]{2,1,0:T(4,128)S(1)} %get-tuple-element.242), channel_id=1, source_target_pairs={{0,1},{1,2},{2,3},{3,0},{4,5},{5,6},{6,7},{7,4},{8,9},{9,10},{10,1... | collective-permute-start | bytes 82952 | tf_op jit(solution)/shard_map/ppermute | solution.py:14
where the time goes:
time: 333 us; the launch traced here: 328 us
  blocking collectives  126 us (38%)
  other arithmetic  60.4 us (18%)
  matrix products  54.6 us (16%)
  starting transfers between devices  45.5 us (14%)
  waiting for transfers between devices  28.1 us (8%)
  between operations  11.7 us (4%)
    psum x12, blocking collectives, one_axis_at_a_time(): shard = lax.psum(shard, axis)  126 us
    dot_general x3, matrix products, spread_dense(): jnp.einsum('cxym,mz->cxyz', weighted, table_z, precision=lax.Precision.HI...  48.7 us
    ppermute x24, starting transfers between devices, shifted(): lax.ppermute(shard, axis, [(i, (i + by) % length) for i in range(length)])  37.1 us
    reduce_sum x6, other arithmetic, axis_rows(): return jnp.sum(delta_weights(fraction)[:, :, None] * hits, axis=0)  37 us
    ppermute x24, waiting for transfers between devices, shifted(): lax.ppermute(shard, axis, [(i, (i + by) % length) for i in range(length)])  18.6 us
    ppermute x3, waiting for transfers between devices, extended(): lax.ppermute(tail, axis, [(i, (i + 1) % count) for i in range(count)])  8.6 us
    mul x15, other arithmetic, stream_wide(): 3.0 * share * (along_x * piece[0] + along_y * piece[1] + along_z * piece[2])  7.43 us
    ppermute x3, starting transfers between devices, extended(): lax.ppermute(head, axis, [((i + 1) % count, i) for i in range(count)])  6.7 us
  transfers between devices with their start and end apart: 30, of which 15 were waited for; matrix products, arithmetic and copies ran while one was open for 14% of the time, Pallas kernels for 0%

commit v1 on v0

--- a/solution.py
+++ b/solution.py
@@ -32,7 +32,7 @@
 
 def one_axis_at_a_time(shard, axes):
     for axis in axes:
-        shard = lax.psum(shard, axis)
+        shard = lax.all_gather(shard, axis).sum(axis=0)
     return shard
 
 

time: 333 us -> 375 us (1.13)
  local copies, waits for them, and re-layouts: 1.68 us -> 36.4 us
  other arithmetic: 60.4 us -> 75.1 us
  blocking collectives: 126 us -> 118 us
    psum x12 -> x0, blocking collectives: 126 us -> none  [one_axis_at_a_time(): shard = lax.psum(shard, axis)]
    unnamed x0 -> x12, blocking collectives: none -> 118 us
    unnamed x27 -> x85, local copies, waits for them, and re-layouts: 0.16 us -> 34.9 us
    reduce_sum x0 -> x24, other arithmetic: none -> 14.8 us  [one_axis_at_a_time(): shard = lax.all_gather(shard, axis).sum(axis=0)]
  transfers between devices with their start and end apart: 30 -> 30, of which waited for: 15 -> 15; matrix products, arithmetic and copies ran while one was open for 14% -> 12% of each run, Pallas kernels for 0% -> 0%
where the time goes in v1:
time: 375 us; the launch traced here: 369 us
  blocking collectives  118 us (31%)
  other arithmetic  75.1 us (20%)
  matrix products  54.4 us (15%)
  starting transfers between devices  45.8 us (12%)
  local copies, waits for them, and re-layouts  36.4 us (10%)
  waiting for transfers between devices  28 us (7%)
  between operations  11.7 us (3%)
    unnamed x12, blocking collectives  118 us
    dot_general x3, matrix products, spread_dense(): jnp.einsum('cxym,mz->cxyz', weighted, table_z, precision=lax.Precision.HI...  48.5 us
    ppermute x24, starting transfers between devices, shifted(): lax.ppermute(shard, axis, [(i, (i + by) % length) for i in range(length)])  37.5 us
    reduce_sum x6, other arithmetic, axis_rows(): return jnp.sum(delta_weights(fraction)[:, :, None] * hits, axis=0)  37 us
    unnamed x85, local copies, waits for them, and re-layouts  34.9 us
    ppermute x24, waiting for transfers between devices, shifted(): lax.ppermute(shard, axis, [(i, (i + by) % length) for i in range(length)])  18.5 us
    reduce_sum x24, other arithmetic, one_axis_at_a_time(): shard = lax.all_gather(shard, axis).sum(axis=0)  14.8 us
    ppermute x3, waiting for transfers between devices, extended(): lax.ppermute(tail, axis, [(i, (i + 1) % count) for i in range(count)])  8.6 us
  transfers between devices with their start and end apart: 30, of which 15 were waited for; matrix products, arithmetic and copies ran while one was open for 12% of the time, Pallas kernels for 0%

profile of v1, /device:TPU:2, one launch (start us, length us, event | category | flops | bytes accessed | tf_op | source)
XLA Modules:
  0.0 369.1 jit_solution(14225757838168493013)
XLA Ops:
  1.5 1.9 collective-permute-start.13
  3.4 4.0 %collective-permute-start.12 = (f32[1,6,256]{2,1,0:T(8,128)S(1)}, f32[1,6,256]{2,1,0:T(8,128)S(1)}, u32[]{:S(2)}, u32[]{:S(2)}) collective-permute-start(f32[1,6,256]{2,1,0:T(8,128)S(1)} %maximum_bitcast_fusion), channel_id=1, source_target_pairs={{0,224},{32,0},{64,32},{96,64},{128,96},{160,128},{192,160},{224,1... | collective-permute-start | bytes 18440 | tf_op jit(solution)/shard_map/ppermute | solution.py:14
  9.1 3.2 collective-permute-start.1
  16.4 2.9 collective-permute-start.14
  19.4 1.5 collective-permute-done.14
  20.9 1.6 collective-permute-start.17
  24.2 2.9 collective-permute-start.3
  30.0 34.5 %select_reduce_fusion = f32[6912,134]{0,1:T(8,128)S(1)} fusion(f32[4,6912]{1,0:T(4,128)S(1)} %pad_maximum_fusion.5, s32[4,6912]{1,0:T(4,128)S(1)} %add_add_fusion), kind=kLoop, calls=%fused_computation.6 | loop fusion | flops 10188288 | bytes 3926016 | tf_op jit(solution)/shard_map/reduce_sum | solution.py:70
  66.2 1.6 collective-permute-start.4
  69.3 8.6 %collective-permute-done.4 = f32[4,14,14,3]{3,2,1,0:T(8,128)S(1)} collective-permute-done((f32[4,14,14,3]{3,2,1,0:T(8,128)S(1)}, f32[4,14,14,3]{3,2,1,0:T(8,128)S(1)}, u32[]{:S(2)}, u32[]{:S(2)}) %collective-permute-start.4) | collective-permute-done | bytes 9440 | tf_op jit(solution)/shard_map/ppermute | solution.py:24
  80.3 3.2 collective-permute-start.6
  83.5 1.6 collective-permute-done.7
  85.1 2.9 collective-permute-start.8
  88.1 1.4 collective-permute-done.8
  90.6 1.7 collective-permute-start.11
  92.3 1.5 collective-permute-done.10
  93.8 2.3 collective-permute-done.11
  96.2 14.8 %fusion.15 = f32[3,14,14,134]{3,2,1,0:T(8,128)S(1)} fusion(f32[6912,134]{0,1:T(8,128)S(1)} %select_reduce_fusion, f32[14,6912]{1,0:T(8,128)S(1)} %bitcast.106, f32[3,14,6912]{2,1,0:T(8,128)S(1)} %broadcast_multiply_fusion.2, f32[14,14,134]{2,1,0:T(8,128)S(1)} %slice_bitcast_fusion), kind=kOutput, calls=%fused_computation.21 | convolution fusion | flops 6539466752 | bytes 5673344 | tf_op jit(solution)/shard_map/cxym,mz->cxyz/dot_general | solution.py:83
  115.2 1.7 fusion.31
  117.5 1.3 dynamic-update-slice.4
  120.6 17.3 %all-reduce.26 = (f32[8]{0:T(128)S(1)}, f32[8]{0:T(128)S(1)}) all-reduce(f32[8]{0:T(128)S(1)} %dynamic-update-slice, f32[8]{0:T(128)S(1)} %dynamic-update-slice.4), channel_id=1, replica_groups=mesh['gx'=8,'gy_0'=4,'gy_1'=2,'gz'=4] {'gx'}, use_global_device_ids=true, to_apply=%add | all-reduce | flops 16 | bytes 128
  139.2 1.3 dynamic-update-slice.5
  140.5 1.3 dynamic-update-slice.1
  142.5 9.6 %all-reduce.32 = (f32[4]{0:T(128)S(1)}, f32[4]{0:T(128)S(1)}) all-reduce(f32[4]{0:T(128)S(1)} %dynamic-update-slice.1, f32[4]{0:T(128)S(1)} %dynamic-update-slice.5), channel_id=1, replica_groups=mesh['gx'=8,'gy_0'=4,'gy_1'=2,'gz'=4] {'gy_0'}, use_global_device_ids=true, to_apply=%add.1 | all-reduce | flops 8 | bytes 64
  153.3 1.3 dynamic-update-slice.6
  154.6 1.4 dynamic-update-slice.2
  156.6 2.4 all-reduce.35
  160.3 1.4 dynamic-update-slice.7
  161.7 1.4 dynamic-update-slice.3
  163.1 11.1 %all-reduce.29 = (f32[4]{0:T(128)S(1)}, f32[4]{0:T(128)S(1)}) all-reduce(f32[4]{0:T(128)S(1)} %dynamic-update-slice.3, f32[4]{0:T(128)S(1)} %dynamic-update-slice.7), channel_id=1, replica_groups=mesh['gx'=8,'gy_0'=4,'gy_1'=2,'gz'=4] {'gz'}, use_global_device_ids=true, to_apply=%add.3 | all-reduce | flops 8 | bytes 64
  177.0 3.2 collective-permute-start.18
  180.2 1.6 collective-permute-done.19
  181.8 2.9 collective-permute-start.20
  184.8 1.4 collective-permute-done.20
  186.7 2.0 collective-permute-start.23
  188.7 1.9 collective-permute-done.22
  190.8 16.8 %fusion.20 = f32[3,14,14,134]{3,2,1,0:T(8,128)S(1)} fusion(f32[6912,134]{0,1:T(8,128)} %copy-done, f32[3,14,6912]{2,1,0:T(8,128)S(1)} %broadcast_multiply_fusion.1, f32[14,6912]{1,0:T(8,128)S(1)} %bitcast.107, f32[14,14,134]{2,1,0:T(8,128)S(1)} %slice_bitcast_fusion), kind=kOutput, calls=%fused_computation.22 | convolution fusion | flops 6539466752 | bytes 5673344 | tf_op jit(solution)/shard_map/cxym,mz->cxyz/dot_general | solution.py:83
  211.8 1.7 fusion.32
  216.7 17.3 %all-reduce.25 = (f32[8]{0:T(128)S(1)}, f32[8]{0:T(128)S(1)}) all-reduce(f32[8]{0:T(128)S(1)} %dynamic-update-slice.8, f32[8]{0:T(128)S(1)} %dynamic-update-slice.12), channel_id=1, replica_groups=mesh['gx'=8,'gy_0'=4,'gy_1'=2,'gz'=4] {'gx'}, use_global_device_ids=true, to_apply=%add.8 | all-reduce | flops 16 | bytes 128
  237.8 7.7 %all-reduce.31 = (f32[4]{0:T(128)S(1)}, f32[4]{0:T(128)S(1)}) all-reduce(f32[4]{0:T(128)S(1)} %dynamic-update-slice.9, f32[4]{0:T(128)S(1)} %dynamic-update-slice.13), channel_id=1, replica_groups=mesh['gx'=8,'gy_0'=4,'gy_1'=2,'gz'=4] {'gy_0'}, use_global_device_ids=true, to_apply=%add.9 | all-reduce | flops 8 | bytes 64
  246.1 1.3 dynamic-update-slice.14
  248.0 1.3 dynamic-update-slice.10
  249.3 2.4 all-reduce.34
  255.5 10.8 %all-reduce.28 = (f32[4]{0:T(128)S(1)}, f32[4]{0:T(128)S(1)}) all-reduce(f32[4]{0:T(128)S(1)} %dynamic-update-slice.11, f32[4]{0:T(128)S(1)} %dynamic-update-slice.15), channel_id=1, replica_groups=mesh['gx'=8,'gy_0'=4,'gy_1'=2,'gz'=4] {'gz'}, use_global_device_ids=true, to_apply=%add.11 | all-reduce | flops 8 | bytes 64
  272.2 3.2 collective-permute-start.24
  275.4 1.6 collective-permute-done.25
  277.0 2.9 collective-permute-start.26
  280.0 1.4 collective-permute-done.26
  281.7 2.0 collective-permute-start.29
  283.7 2.2 collective-permute-done.28
  286.1 16.9 %fusion.25 = f32[3,14,14,134]{3,2,1,0:T(8,128)S(1)} fusion(f32[6912,134]{0,1:T(8,128)} %copy-done, f32[3,14,6912]{2,1,0:T(8,128)S(1)} %broadcast_multiply_fusion, f32[14,6912]{1,0:T(8,128)S(1)} %bitcast.108, f32[14,14,134]{2,1,0:T(8,128)S(1)} %slice_bitcast_fusion), kind=kOutput, calls=%fused_computation.23 | convolution fusion | flops 6539466752 | bytes 5673344 | tf_op jit(solution)/shard_map/cxym,mz->cxyz/dot_general | solution.py:83
  307.2 1.8 fusion.33
  309.6 1.3 dynamic-update-slice.20
  310.9 1.3 dynamic-update-slice.16
  312.3 17.4 %all-reduce.24 = (f32[8]{0:T(128)S(1)}, f32[8]{0:T(128)S(1)}) all-reduce(f32[8]{0:T(128)S(1)} %dynamic-update-slice.16, f32[8]{0:T(128)S(1)} %dynamic-update-slice.20), channel_id=1, replica_groups=mesh['gx'=8,'gy_0'=4,'gy_1'=2,'gz'=4] {'gx'}, use_global_device_ids=true, to_apply=%add.16 | all-reduce | flops 16 | bytes 128
  330.2 1.3 dynamic-update-slice.21
  332.1 1.3 dynamic-update-slice.17
  333.5 8.2 %all-reduce.30 = (f32[4]{0:T(128)S(1)}, f32[4]{0:T(128)S(1)}) all-reduce(f32[4]{0:T(128)S(1)} %dynamic-update-slice.17, f32[4]{0:T(128)S(1)} %dynamic-update-slice.21), channel_id=1, replica_groups=mesh['gx'=8,'gy_0'=4,'gy_1'=2,'gz'=4] {'gy_0'}, use_global_device_ids=true, to_apply=%add.17 | all-reduce | flops 8 | bytes 64
  342.3 1.4 dynamic-update-slice.22
  344.2 1.4 dynamic-update-slice.18
  345.6 2.4 all-reduce.33
  348.7 1.4 dynamic-update-slice.23
  350.6 1.4 dynamic-update-slice.19
  352.0 10.8 %all-reduce.27 = (f32[4]{0:T(128)S(1)}, f32[4]{0:T(128)S(1)}) all-reduce(f32[4]{0:T(128)S(1)} %dynamic-update-slice.19, f32[4]{0:T(128)S(1)} %dynamic-update-slice.23), channel_id=1, replica_groups=mesh['gx'=8,'gy_0'=4,'gy_1'=2,'gz'=4] {'gz'}, use_global_device_ids=true, to_apply=%add.19 | all-reduce | flops 8 | bytes 64
  (223 shorter events, 59.5 us)
Async XLA Ops:
  1.5 14.9 %collective-permute-start.13 = (f32[1,6,256]{2,1,0:T(8,128)S(1)}, f32[1,6,256]{2,1,0:T(8,128)S(1)}, u32[]{:S(2)}, u32[]{:S(2)}) collective-permute-start(f32[1,6,256]{2,1,0:T(8,128)S(1)} %maximum_bitcast_fusion), channel_id=1, source_target_pairs={{0,32},{32,64},{64,96},{96,128},{128,160},{160,192},{192,224},{224... | collective-permute-start | bytes 18440 | tf_op jit(solution)/shard_map/ppermute | solution.py:14
  3.4 13.0 %collective-permute-start.12 = (f32[1,6,256]{2,1,0:T(8,128)S(1)}, f32[1,6,256]{2,1,0:T(8,128)S(1)}, u32[]{:S(2)}, u32[]{:S(2)}) collective-permute-start(f32[1,6,256]{2,1,0:T(8,128)S(1)} %maximum_bitcast_fusion), channel_id=1, source_target_pairs={{0,224},{32,0},{64,32},{96,64},{128,96},{160,128},{192,160},{224,1... | collective-permute-start | bytes 18440 | tf_op jit(solution)/shard_map/ppermute | solution.py:14
  9.0 14.2 %collective-permute-start = (f32[4,3,8,128]{3,2,1,0:T(8,128)S(1)}, f32[4,3,8,128]{3,2,1,0:T(8,128)S(1)}, u32[]{:S(2)}, u32[]{:S(2)}) collective-permute-start(f32[4,3,8,128]{3,2,1,0:T(8,128)S(1)} %get-tuple-element.221), channel_id=1, source_target_pairs={{0,32},{32,64},{64,96},{96,128},{128,160},{160,192},{192,224},{224... | collective-permute-start | bytes 147464 | tf_op jit(solution)/shard_map/ppermute | solution.py:24
  9.1 14.1 %collective-permute-start.1 = (f32[4,3,8,128]{3,2,1,0:T(8,128)S(1)}, f32[4,3,8,128]{3,2,1,0:T(8,128)S(1)}, u32[]{:S(2)}, u32[]{:S(2)}) collective-permute-start(f32[4,3,8,128]{3,2,1,0:T(8,128)S(1)} %get-tuple-element.222), channel_id=1, source_target_pairs={{32,0},{64,32},{96,64},{128,96},{160,128},{192,160},{224,192},{0,2... | collective-permute-start | bytes 147464 | tf_op jit(solution)/shard_map/ppermute | solution.py:26
  16.4 4.5 %collective-permute-start.15 = (f32[3,6,256]{2,1,0:T(8,128)S(1)}, f32[3,6,256]{2,1,0:T(8,128)S(1)}, u32[]{:S(2)}, u32[]{:S(2)}) collective-permute-start(f32[3,6,256]{2,1,0:T(8,128)S(1)} %pad_maximum_fusion.8), channel_id=1, source_target_pairs={{0,4},{4,8},{8,12},{12,16},{16,20},{20,24},{24,28},{28,0},{1,5},{5... | collective-permute-start | bytes 55304 | tf_op jit(solution)/shard_map/ppermute | solution.py:14
  16.4 4.5 %collective-permute-start.14 = (f32[3,6,256]{2,1,0:T(8,128)S(1)}, f32[3,6,256]{2,1,0:T(8,128)S(1)}, u32[]{:S(2)}, u32[]{:S(2)}) collective-permute-start(f32[3,6,256]{2,1,0:T(8,128)S(1)} %pad_maximum_fusion.8), channel_id=1, source_target_pairs={{0,28},{4,0},{8,4},{12,8},{16,12},{20,16},{24,20},{28,24},{1,29},{... | collective-permute-start | bytes 55304 | tf_op jit(solution)/shard_map/ppermute | solution.py:14
  20.9 6.3 %collective-permute-start.17 = (f32[9,6,256]{2,1,0:T(8,128)S(1)}, f32[9,6,256]{2,1,0:T(8,128)S(1)}, u32[]{:S(2)}, u32[]{:S(2)}) collective-permute-start(f32[9,6,256]{2,1,0:T(8,128)S(1)} %get-tuple-element.238), channel_id=1, source_target_pairs={{0,1},{1,2},{2,3},{3,0},{4,5},{5,6},{6,7},{7,4},{8,9},{9,10},{10,1... | collective-permute-start | bytes 165896 | tf_op jit(solution)/shard_map/ppermute | solution.py:14
  22.5 4.7 %collective-permute-start.16 = (f32[9,6,256]{2,1,0:T(8,128)S(1)}, f32[9,6,256]{2,1,0:T(8,128)S(1)}, u32[]{:S(2)}, u32[]{:S(2)}) collective-permute-start(f32[9,6,256]{2,1,0:T(8,128)S(1)} %get-tuple-element.238), channel_id=1, source_target_pairs={{0,3},{1,0},{2,1},{3,2},{4,7},{5,4},{6,5},{7,6},{8,11},{9,8},{10,9... | collective-permute-start | bytes 165896 | tf_op jit(solution)/shard_map/ppermute | solution.py:14
  24.2 41.7 %collective-permute-start.2 = (f32[4,14,3,128]{3,2,1,0:T(4,128)S(1)}, f32[4,14,3,128]{3,2,1,0:T(4,128)S(1)}, u32[]{:S(2)}, u32[]{:S(2)}) collective-permute-start(f32[4,14,3,128]{3,2,1,0:T(4,128)S(1)} %get-tuple-element.183), channel_id=1, source_target_pairs={{0,4},{4,8},{8,12},{12,16},{16,20},{20,24},{24,28},{28,0},{1,5},{5... | collective-permute-start | bytes 258056 | tf_op jit(solution)/shard_map/ppermute | solution.py:24
  24.2 41.6 %collective-permute-start.3 = (f32[4,14,3,128]{3,2,1,0:T(4,128)S(1)}, f32[4,14,3,128]{3,2,1,0:T(4,128)S(1)}, u32[]{:S(2)}, u32[]{:S(2)}) collective-permute-start(f32[4,14,3,128]{3,2,1,0:T(4,128)S(1)} %get-tuple-element.184), channel_id=1, source_target_pairs={{4,0},{8,4},{12,8},{16,12},{20,16},{24,20},{28,24},{0,28},{5,1},{9... | collective-permute-start | bytes 258056 | tf_op jit(solution)/shard_map/ppermute | solution.py:26
  27.2 38.7 %copy-start.1 = (f32[3,8,8,128]{3,2,1,0:T(8,128)S(1)}, f32[3,8,8,128]{3,2,1,0:T(8,128)}, u32[]{:S(2)}) copy-start(f32[3,8,8,128]{3,2,1,0:T(8,128)} %param.10) | copy-start | bytes 294916
  64.6 31.6 %copy-start = (f32[6912,134]{0,1:T(8,128)}, f32[6912,134]{0,1:T(8,128)S(1)}, u32[]{:S(2)}) copy-start(f32[6912,134]{0,1:T(8,128)S(1)} %select_reduce_fusion) | copy-start | bytes 11114500
  64.8 15.4 %copy-start.3 = (f32[3,256]{1,0:T(4,128)S(1)}, f32[3,256]{1,0:T(4,128)}, u32[]{:S(2)}) copy-start(f32[3,256]{1,0:T(4,128)} %param.13) | copy-start | bytes 9220
  66.2 11.7 %collective-permute-start.4 = (f32[4,14,14,3]{3,2,1,0:T(8,128)S(1)}, f32[4,14,14,3]{3,2,1,0:T(8,128)S(1)}, u32[]{:S(2)}, u32[]{:S(2)}) collective-permute-start(f32[4,14,14,3]{3,2,1,0:T(8,128)S(1)} %get-tuple-element.181), channel_id=1, source_target_pairs={{0,1},{1,2},{2,3},{3,0},{4,5},{5,6},{6,7},{7,4},{8,9},{9,10},{10,1... | collective-permute-start | bytes 28232 | tf_op jit(solution)/shard_map/ppermute | solution.py:24
  67.7 11.1 %collective-permute-start.5 = (f32[4,14,14,3]{3,2,1,0:T(8,128)S(1)}, f32[4,14,14,3]{3,2,1,0:T(8,128)S(1)}, u32[]{:S(2)}, u32[]{:S(2)}) collective-permute-start(f32[4,14,14,3]{3,2,1,0:T(8,128)S(1)} %get-tuple-element.182), channel_id=1, source_target_pairs={{1,0},{2,1},{3,2},{0,3},{5,4},{6,5},{7,6},{4,7},{9,8},{10,9},{11,1... | collective-permute-start | bytes 28232 | tf_op jit(solution)/shard_map/ppermute | solution.py:26
  80.2 4.9 %collective-permute-start.7 = (f32[1,3,256]{2,1,0:T(4,128)S(1)}, f32[1,3,256]{2,1,0:T(4,128)S(1)}, u32[]{:S(2)}, u32[]{:S(2)}) collective-permute-start(f32[1,3,256]{2,1,0:T(4,128)S(1)} %bitcast.109), channel_id=1, source_target_pairs={{0,32},{32,64},{64,96},{96,128},{128,160},{160,192},{192,224},{224... | collective-permute-start | bytes 9224 | tf_op jit(solution)/shard_map/ppermute | solution.py:14
  80.3 4.8 %collective-permute-start.6 = (f32[1,3,256]{2,1,0:T(4,128)S(1)}, f32[1,3,256]{2,1,0:T(4,128)S(1)}, u32[]{:S(2)}, u32[]{:S(2)}) collective-permute-start(f32[1,3,256]{2,1,0:T(4,128)S(1)} %bitcast.110), channel_id=1, source_target_pairs={{0,224},{32,0},{64,32},{96,64},{128,96},{160,128},{192,160},{224,1... | collective-permute-start | bytes 9224 | tf_op jit(solution)/shard_map/ppermute | solution.py:14
  85.1 4.4 %collective-permute-start.9 = (f32[3,3,256]{2,1,0:T(4,128)S(1)}, f32[3,3,256]{2,1,0:T(4,128)S(1)}, u32[]{:S(2)}, u32[]{:S(2)}) collective-permute-start(f32[3,3,256]{2,1,0:T(4,128)S(1)} %pad_maximum_fusion.9), channel_id=1, source_target_pairs={{0,4},{4,8},{8,12},{12,16},{16,20},{20,24},{24,28},{28,0},{1,5},{5... | collective-permute-start | bytes 27656 | tf_op jit(solution)/shard_map/ppermute | solution.py:14
  85.1 4.3 %collective-permute-start.8 = (f32[3,3,256]{2,1,0:T(4,128)S(1)}, f32[3,3,256]{2,1,0:T(4,128)S(1)}, u32[]{:S(2)}, u32[]{:S(2)}) collective-permute-start(f32[3,3,256]{2,1,0:T(4,128)S(1)} %pad_maximum_fusion.9), channel_id=1, source_target_pairs={{0,28},{4,0},{8,4},{12,8},{16,12},{20,16},{24,20},{28,24},{1,29},{... | collective-permute-start | bytes 27656 | tf_op jit(solution)/shard_map/ppermute | solution.py:14
  89.5 4.3 %collective-permute-start.10 = (f32[9,3,256]{2,1,0:T(4,128)S(1)}, f32[9,3,256]{2,1,0:T(4,128)S(1)}, u32[]{:S(2)}, u32[]{:S(2)}) collective-permute-start(f32[9,3,256]{2,1,0:T(4,128)S(1)} %get-tuple-element.250), channel_id=1, source_target_pairs={{0,3},{1,0},{2,1},{3,2},{4,7},{5,4},{6,5},{7,6},{8,11},{9,8},{10,9... | collective-permute-start | bytes 82952 | tf_op jit(solution)/shard_map/ppermute | solution.py:14
  90.6 5.5 %collective-permute-start.11 = (f32[9,3,256]{2,1,0:T(4,128)S(1)}, f32[9,3,256]{2,1,0:T(4,128)S(1)}, u32[]{:S(2)}, u32[]{:S(2)}) collective-permute-start(f32[9,3,256]{2,1,0:T(4,128)S(1)} %get-tuple-element.250), channel_id=1, source_target_pairs={{0,1},{1,2},{2,3},{3,0},{4,5},{5,6},{6,7},{7,4},{8,9},{9,10},{10,1... | collective-permute-start | bytes 82952 | tf_op jit(solution)/shard_map/ppermute | solution.py:14
  115.1 1.8 copy-start.2
  115.1 4.9 %copy-start.6 = (u32[256]{0:T(256)S(1)}, u32[256]{0:T(256)}, u32[]{:S(2)}) copy-start(u32[256]{0:T(256)} %constant.199) | copy-start | bytes 3076
  115.1 26.7 %copy-start.5 = (u32[256]{0:T(256)S(1)}, u32[256]{0:T(256)}, u32[]{:S(2)}) copy-start(u32[256]{0:T(256)} %constant.204) | copy-start | bytes 3076
  115.2 40.8 %copy-start.4 = (u32[256]{0:T(256)S(1)}, u32[256]{0:T(256)}, u32[]{:S(2)}) copy-start(u32[256]{0:T(256)} %constant.209) | copy-start | bytes 3076
  176.9 4.9 %collective-permute-start.19 = (f32[1,3,256]{2,1,0:T(4,128)S(1)}, f32[1,3,256]{2,1,0:T(4,128)S(1)}, u32[]{:S(2)}, u32[]{:S(2)}) collective-permute-start(f32[1,3,256]{2,1,0:T(4,128)S(1)} %bitcast.112), channel_id=1, source_target_pairs={{0,32},{32,64},{64,96},{96,128},{128,160},{160,192},{192,224},{224... | collective-permute-start | bytes 9224 | tf_op jit(solution)/shard_map/ppermute | solution.py:14
  177.0 4.8 %collective-permute-start.18 = (f32[1,3,256]{2,1,0:T(4,128)S(1)}, f32[1,3,256]{2,1,0:T(4,128)S(1)}, u32[]{:S(2)}, u32[]{:S(2)}) collective-permute-start(f32[1,3,256]{2,1,0:T(4,128)S(1)} %bitcast.113), channel_id=1, source_target_pairs={{0,224},{32,0},{64,32},{96,64},{128,96},{160,128},{192,160},{224,1... | collective-permute-start | bytes 9224 | tf_op jit(solution)/shard_map/ppermute | solution.py:14
  181.8 4.4 %collective-permute-start.21 = (f32[3,3,256]{2,1,0:T(4,128)S(1)}, f32[3,3,256]{2,1,0:T(4,128)S(1)}, u32[]{:S(2)}, u32[]{:S(2)}) collective-permute-start(f32[3,3,256]{2,1,0:T(4,128)S(1)} %pad_maximum_fusion.10), channel_id=1, source_target_pairs={{0,4},{4,8},{8,12},{12,16},{16,20},{20,24},{24,28},{28,0},{1,5},{5... | collective-permute-start | bytes 27656 | tf_op jit(solution)/shard_map/ppermute | solution.py:14
  181.8 4.3 %collective-permute-start.20 = (f32[3,3,256]{2,1,0:T(4,128)S(1)}, f32[3,3,256]{2,1,0:T(4,128)S(1)}, u32[]{:S(2)}, u32[]{:S(2)}) collective-permute-start(f32[3,3,256]{2,1,0:T(4,128)S(1)} %pad_maximum_fusion.10), channel_id=1, source_target_pairs={{0,28},{4,0},{8,4},{12,8},{16,12},{20,16},{24,20},{28,24},{1,29},{... | collective-permute-start | bytes 27656 | tf_op jit(solution)/shard_map/ppermute | solution.py:14
  186.2 4.4 %collective-permute-start.22 = (f32[9,3,256]{2,1,0:T(4,128)S(1)}, f32[9,3,256]{2,1,0:T(4,128)S(1)}, u32[]{:S(2)}, u32[]{:S(2)}) collective-permute-start(f32[9,3,256]{2,1,0:T(4,128)S(1)} %get-tuple-element.246), channel_id=1, source_target_pairs={{0,3},{1,0},{2,1},{3,2},{4,7},{5,4},{6,5},{7,6},{8,11},{9,8},{10,9... | collective-permute-start | bytes 82952 | tf_op jit(solution)/shard_map/ppermute | solution.py:14
  186.7 4.0 %collective-permute-start.23 = (f32[9,3,256]{2,1,0:T(4,128)S(1)}, f32[9,3,256]{2,1,0:T(4,128)S(1)}, u32[]{:S(2)}, u32[]{:S(2)}) collective-permute-start(f32[9,3,256]{2,1,0:T(4,128)S(1)} %get-tuple-element.246), channel_id=1, source_target_pairs={{0,1},{1,2},{2,3},{3,0},{4,5},{5,6},{6,7},{7,4},{8,9},{9,10},{10,1... | collective-permute-start | bytes 82952 | tf_op jit(solution)/shard_map/ppermute | solution.py:14
  272.1 4.9 %collective-permute-start.25 = (f32[1,3,256]{2,1,0:T(4,128)S(1)}, f32[1,3,256]{2,1,0:T(4,128)S(1)}, u32[]{:S(2)}, u32[]{:S(2)}) collective-permute-start(f32[1,3,256]{2,1,0:T(4,128)S(1)} %bitcast.121), channel_id=1, source_target_pairs={{0,32},{32,64},{64,96},{96,128},{128,160},{160,192},{192,224},{224... | collective-permute-start | bytes 9224 | tf_op jit(solution)/shard_map/ppermute | solution.py:14
  272.2 4.8 %collective-permute-start.24 = (f32[1,3,256]{2,1,0:T(4,128)S(1)}, f32[1,3,256]{2,1,0:T(4,128)S(1)}, u32[]{:S(2)}, u32[]{:S(2)}) collective-permute-start(f32[1,3,256]{2,1,0:T(4,128)S(1)} %bitcast.122), channel_id=1, source_target_pairs={{0,224},{32,0},{64,32},{96,64},{128,96},{160,128},{192,160},{224,1... | collective-permute-start | bytes 9224 | tf_op jit(solution)/shard_map/ppermute | solution.py:14
  277.0 4.4 %collective-permute-start.27 = (f32[3,3,256]{2,1,0:T(4,128)S(1)}, f32[3,3,256]{2,1,0:T(4,128)S(1)}, u32[]{:S(2)}, u32[]{:S(2)}) collective-permute-start(f32[3,3,256]{2,1,0:T(4,128)S(1)} %pad_maximum_fusion.11), channel_id=1, source_target_pairs={{0,4},{4,8},{8,12},{12,16},{16,20},{20,24},{24,28},{28,0},{1,5},{5... | collective-permute-start | bytes 27656 | tf_op jit(solution)/shard_map/ppermute | solution.py:14
  277.0 4.3 %collective-permute-start.26 = (f32[3,3,256]{2,1,0:T(4,128)S(1)}, f32[3,3,256]{2,1,0:T(4,128)S(1)}, u32[]{:S(2)}, u32[]{:S(2)}) collective-permute-start(f32[3,3,256]{2,1,0:T(4,128)S(1)} %pad_maximum_fusion.11), channel_id=1, source_target_pairs={{0,28},{4,0},{8,4},{12,8},{16,12},{20,16},{24,20},{28,24},{1,29},{... | collective-permute-start | bytes 27656 | tf_op jit(solution)/shard_map/ppermute | solution.py:14
  281.4 4.6 %collective-permute-start.28 = (f32[9,3,256]{2,1,0:T(4,128)S(1)}, f32[9,3,256]{2,1,0:T(4,128)S(1)}, u32[]{:S(2)}, u32[]{:S(2)}) collective-permute-start(f32[9,3,256]{2,1,0:T(4,128)S(1)} %get-tuple-element.242), channel_id=1, source_target_pairs={{0,3},{1,0},{2,1},{3,2},{4,7},{5,4},{6,5},{7,6},{8,11},{9,8},{10,9... | collective-permute-start | bytes 82952 | tf_op jit(solution)/shard_map/ppermute | solution.py:14
  281.7 4.3 %collective-permute-start.29 = (f32[9,3,256]{2,1,0:T(4,128)S(1)}, f32[9,3,256]{2,1,0:T(4,128)S(1)}, u32[]{:S(2)}, u32[]{:S(2)}) collective-permute-start(f32[9,3,256]{2,1,0:T(4,128)S(1)} %get-tuple-element.242), channel_id=1, source_target_pairs={{0,1},{1,2},{2,3},{3,0},{4,5},{5,6},{6,7},{7,4},{8,9},{9,10},{10,1... | collective-permute-start | bytes 82952 | tf_op jit(solution)/shard_map/ppermute | solution.py:14
